TPU v7x, 32 devices: a whole 2x2x4 slice. The times are simulated.
32 devices in a mesh: rep: 8 (over y, x, core), tp: 4 (over z).
Axes of the slice: x: 2, y: 2, z: 4, core: 2. Of those that a mesh axis runs over, the one named last changes fastest.
Arguments:
- tokens: bfloat16 [4096, 8192], P('rep'), may hold values from -6 to 6
- query_weight: float32 [8192, 8192], P(('rep', 'tp')), may hold values from -0.0625 to 0.0625
- key_weight: float32 [8192, 1024], P(('rep', 'tp')), may hold values from -0.0625 to 0.0625
- value_weight: float32 [8192, 1024], P(('rep', 'tp')), may hold values from -0.0625 to 0.0625
- cache_keys: bfloat16 [256, 128, 1024], P('rep', None, 'tp'), may hold values from -240 to 240
- cache_values: bfloat16 [256, 128, 1024], P('rep', None, 'tp'), may hold values from -6 to 6
- lengths: int32 [8, 2], P('rep'), may hold values from 1 to 2048
- page_table: int32 [8, 2, 16], P('rep'), may hold values from 0 to 31, as said below
Outputs:
- attended: bfloat16 [4096, 8192], P('rep', 'tp')
- new_cache: bfloat16 [2, 4096, 1024], P(None, 'rep', 'tp')
Inputs may be any that keep to these rules, and one draw needn't show every extreme that they name: For each group g, the 2 x 16 entries of page_table[g] name each of the group's local pool pages 0 to 31 exactly once.
All inputs are finite; a program needn't handle non-finite values.
Results may differ from a plain program's by a relative error of at most 0.008.
The roundings to bfloat16 on the way count: a program that leaves them out, or rounds other values in their place, can miss the bound.
Values may be sent and summed in bfloat16 or wider, within the bound.
A program may use at most 192 MiB of HBM per device.

v0:
```python
import jax
import jax.numpy as jnp
from jax import lax
from jax.sharding import PartitionSpec as P

HEADS = 64
KV_HEADS = 8
HEAD_DIM = 128
SEQS = 2
NEW = 256
TOK = 512
MAXLEN = 2048
ROPE_THETA = 500000.0


def rotate(vectors, positions):
    half_dim = HEAD_DIM // 2
    frequency = ROPE_THETA ** (-2.0 * jnp.arange(half_dim, dtype=jnp.float32) / HEAD_DIM)
    angles = positions.astype(jnp.float32)[:, None] * frequency[None, :]
    cosine_part = jnp.cos(angles)[:, None, :]
    sine_part = jnp.sin(angles)[:, None, :]
    first_half = vectors[..., :half_dim]
    second_half = vectors[..., half_dim:]
    return jnp.concatenate(
        [
            first_half * cosine_part - second_half * sine_part,
            second_half * cosine_part + first_half * sine_part,
        ],
        axis=-1,
    )


def per_device(
    tokens, query_weight, key_weight, value_weight, cache_keys, cache_values, lengths, page_table
):
    weights = (
        query_weight.astype(jnp.bfloat16),
        key_weight.astype(jnp.bfloat16),
        value_weight.astype(jnp.bfloat16),
    )
    slabs = (
        lax.all_to_all(weights[0], "tp", split_axis=1, concat_axis=0, tiled=True),
        lax.all_to_all(weights[1], "tp", split_axis=1, concat_axis=0, tiled=True),
        lax.all_to_all(weights[2], "tp", split_axis=1, concat_axis=0, tiled=True),
    )
    pieces = (
        lax.all_gather(slabs[0], "rep", axis=0, tiled=True),
        lax.all_gather(slabs[1], "rep", axis=0, tiled=True),
        lax.all_gather(slabs[2], "rep", axis=0, tiled=True),
    )
    raw_query, raw_key, raw_value = tuple(
        (jnp.dot(tokens, piece, preferred_element_type=jnp.float32) for piece in pieces)
    )
    kv_local = raw_key.shape[1] // HEAD_DIM
    group_size = HEADS // KV_HEADS
    scale = 1.0 / HEAD_DIM**0.5
    seq_lengths = lengths[0]
    positions = (seq_lengths[:, None] + jnp.arange(NEW, dtype=jnp.int32)[None, :]).reshape(TOK)
    queries = rotate(raw_query.reshape(TOK, kv_local * group_size, HEAD_DIM), positions).astype(
        jnp.bfloat16
    )
    new_keys = rotate(raw_key.reshape(TOK, kv_local, HEAD_DIM), positions).astype(jnp.bfloat16)
    new_values = raw_value.astype(jnp.bfloat16).reshape(TOK, kv_local, HEAD_DIM)

    def one_sequence(inner):
        seq_queries, seq_keys, seq_values, page_rows, length = inner
        old_keys = cache_keys[page_rows].reshape(MAXLEN, kv_local, HEAD_DIM)
        old_values = cache_values[page_rows].reshape(MAXLEN, kv_local, HEAD_DIM)
        all_keys = jnp.concatenate([old_keys, seq_keys], axis=0)
        all_values = jnp.concatenate([old_values, seq_values], axis=0)
        grouped = seq_queries.reshape(NEW, kv_local, group_size, HEAD_DIM)
        scores = (
            jnp.einsum("nkgd,mkd->kgnm", grouped, all_keys, preferred_element_type=jnp.float32)
            * scale
        )
        key_index = jnp.arange(MAXLEN + NEW, dtype=jnp.int32)[None, :]
        query_index = jnp.arange(NEW, dtype=jnp.int32)[:, None]
        visible = jnp.where(
            key_index < MAXLEN, key_index < length, key_index - MAXLEN <= query_index
        )
        scores = jnp.where(visible[None, None], scores, -1e30)
        maxima = jnp.max(scores, axis=-1, keepdims=True)
        expons = jnp.exp(scores - maxima)
        probs = (expons / jnp.sum(expons, axis=-1, keepdims=True)).astype(jnp.bfloat16)
        output = jnp.einsum("kgnm,mkd->nkgd", probs, all_values, preferred_element_type=jnp.float32)
        return output.astype(jnp.bfloat16).reshape(NEW, kv_local * group_size * HEAD_DIM)

    attended = lax.map(
        one_sequence,
        (
            queries.reshape(SEQS, NEW, kv_local * group_size, HEAD_DIM),
            new_keys.reshape(SEQS, NEW, kv_local, HEAD_DIM),
            new_values.reshape(SEQS, NEW, kv_local, HEAD_DIM),
            page_table[0],
            seq_lengths,
        ),
    )
    new_cache = jnp.stack(
        [new_keys.reshape(TOK, kv_local * HEAD_DIM), new_values.reshape(TOK, kv_local * HEAD_DIM)]
    )
    return (attended.reshape(TOK, kv_local * group_size * HEAD_DIM), new_cache)


def solution(mesh):
    return jax.shard_map(
        per_device,
        mesh=mesh,
        in_specs=(
            P("rep", None),
            P(("rep", "tp"), None),
            P(("rep", "tp"), None),
            P(("rep", "tp"), None),
            P("rep", None, "tp"),
            P("rep", None, "tp"),
            P("rep", None),
            P("rep", None, None),
        ),
        out_specs=(P("rep", "tp"), P(None, "rep", "tp")),
        check_vma=False,
    )
```

profile of v0, /device:TPU:0, one launch (start us, length us, event | category | flops | bytes accessed | tf_op | source)
XLA Modules:
  0.0 450.6 jit_solution(10481622972108164320)
XLA Ops:
  7.2 1.5 copy.33
  8.7 20.6 %all_to_all.57 = bf16[256,4,256]{0,2,1:T(8,128)(2,1)S(1)} all-to-all(bf16[256,4,256]{0,2,1:T(8,128)(2,1)S(1)} %bitcast.110), channel_id=1, replica_groups=mesh['rep'=8,'tp'=4] {'tp'}, dimensions={1} | all-to-all | bytes 1048576 | tf_op jit(solution)/shard_map/all_to_all | solution.py:43
  29.4 1.0 copy.34
  30.7 16.6 %all_to_all.58 = bf16[256,4,256]{0,2,1:T(8,128)(2,1)S(1)} all-to-all(bf16[256,4,256]{0,2,1:T(8,128)(2,1)S(1)} %bitcast.111), channel_id=1, replica_groups=mesh['rep'=8,'tp'=4] {'tp'}, dimensions={1} | all-to-all | bytes 1048576 | tf_op jit(solution)/shard_map/all_to_all | solution.py:44
  47.3 1.0 copy.32
  48.3 7.6 %copy.35 = bf16[256,8192]{0,1:T(8,128)(2,1)} copy(f32[256,8192]{1,0:T(8,128)} %param.11) | data formatting | bytes 12582912 | tf_op args[1]
  55.9 97.8 %all_to_all.59 = bf16[256,4,2048]{0,2,1:T(8,128)(2,1)} all-to-all(bf16[256,4,2048]{0,2,1:T(8,128)(2,1)} %bitcast.105), channel_id=1, replica_groups=mesh['rep'=8,'tp'=4] {'tp'}, dimensions={1} | all-to-all | bytes 8388608 | tf_op jit(solution)/shard_map/all_to_all | solution.py:42
  153.8 6.3 %copy.36 = bf16[4,256,2048]{2,1,0:T(8,128)(2,1)} copy(bf16[4,256,2048]{1,2,0:T(8,128)(2,1)} %bitcast.107) | data formatting | bytes 8388608 | tf_op jit(solution)/shard_map/all_to_all | solution.py:42
  160.1 0.6 copy-done.2
  160.8 0.5 multiply_cosine_fusion
  161.4 7.1 %fusion.23 = f32[512,256]{0,1:T(8,128)S(1)} fusion(bf16[512,8192]{1,0:T(8,128)(2,1)} %param.10, bf16[8192,256]{1,0:T(8,128)(2,1)} %all-gather.6.cloned.1.call-done), kind=kOutput, calls=%fused_computation.51 | convolution fusion | flops 2147483648 | bytes 13107200 | tf_op jit(solution)/shard_map/dot_general | solution.py:52
  168.6 0.3 pad_maximum_fusion.2
  169.2 9.0 %convolution_convert_fusion = bf16[512,256]{1,0:T(8,128)(2,1)S(1)} fusion(bf16[512,8192]{1,0:T(8,128)(2,1)} %param.10, bf16[8192,256]{1,0:T(8,128)(2,1)} %all-gather.4.cloned.1.call-done), kind=kOutput, calls=%fused_computation.40 | convolution fusion | flops 2147614720 | bytes 12845056 | tf_op jit(solution)/shard_map/dot_general | solution.py:52
  178.3 0.8 reshape_reshape.3
  179.2 0.8 pad_maximum_fusion.1
  180.0 140.0 %all-gather.8.cloned.1.call-done = bf16[8192,2048]{1,0:T(8,128)(2,1)} async-done(((bf16[1024,2048]{1,0:T(8,128)(2,1)}), bf16[8192,2048]{1,0:T(8,128)(2,1)}) %all-gather.8.cloned.1.call-update) | async-done | bytes 33554448 | tf_op jit(solution)/shard_map/all_gather | solution.py:47
  320.0 25.8 %fusion.24 = f32[512,2048]{0,1:T(8,128)} fusion(bf16[512,8192]{1,0:T(8,128)(2,1)} %param.10, bf16[8192,2048]{1,0:T(8,128)(2,1)} %all-gather.8.cloned.1.call-done), kind=kOutput, calls=%fused_computation.52 | convolution fusion | flops 17179869184 | bytes 46137344 | tf_op jit(solution)/shard_map/reshape | solution.py:59
  345.8 2.9 subtract_convert_fusion
  349.0 1.1 concatenate.37
  350.2 3.9 pad_maximum_fusion
  354.1 3.7 copy.41
  357.8 86.2 %while.12 = (s32[]{:T(128)}, bf16[2,256,2048]{2,1,0:T(8,128)(2,1)}, s32[2,16]{1,0:T(2,128)S(1)}, bf16[32,128,256]{2,1,0:T(8,128)(2,1)}, bf16[2,256,2,128]{3,2,1,...) while((s32[]{:T(128)}, bf16[2,256,2048]{2,1,0:T(8,128)(2,1)}, ...), condition=%wide.region_3.4_spmd, body=%wide.region_0.3_spmd.sunk | while | flops 4894894080 | bytes 100859848 | solution.py:88
  357.8 0.6 dynamic_slice.53
  358.4 0.6 iota_compare_fusion.4
  359.1 1.9 fusion.39
  361.0 2.2 gather_fusion
  363.2 0.3 reshape.269
  363.7 1.3 constant_dynamic-slice_fusion.5
  365.0 17.5 %fusion.41 = (f32[2,8,256]{2,1,0:T(8,128)S(1)}, f32[2,8,256,2304]{2,3,1,0:T(8,128)}) fusion(bf16[256,2,8,128]{3,0,2,1:T(8,128)(2,1)S(1)} %bitcast.103, pred[256,2304]{0,1:T(8,128)(4,1)S(1)} %fusion.39, bf16[256,2,128]{2,0,1:T(8,128)(2,1)S(1)} %dynamic-slice_bitcast_fusion.2, bf16[2048,2,128]{2,0,1:T(8,128)(2,1)S(1)} %copy.60), kind=kOutput, calls=%fused_computation.50.clone.1 | convolution fusion | flops 2456029440 | bytes 40583168 | tf_op jit(solution)/shard_map/while/body/eval_jaxpr/sub | solution.py:83
  382.4 2.2 gather_fusion.1
  384.7 0.3 reshape.270
  384.9 0.8 copy.62
  386.0 13.3 %fusion.42 = bf16[2,128,8,256]{3,1,2,0:T(8,128)(2,1)S(1)} fusion(f32[2,8,256,2304]{2,3,1,0:T(8,128)} %get-tuple-element.232, f32[2,8,256]{2,1,0:T(8,128)S(1)} %get-tuple-element.233, bf16[256,2,128]{0,2,1:T(8,128)(2,1)S(1)} %bitcast.109, bf16[2048,2,128]{0,2,1:T(8,128)(2,1)S(1)} %copy.62), kind=kOutput, calls=%fused_computation.14.clone.1 | convolution fusion | flops 2437677056 | bytes 39993344 | tf_op jit(solution)/shard_map/while/body/eval_jaxpr/kgnm,mkd->nkgd/dot_general | solution.py:85
  399.3 0.6 copy.63
  399.9 1.0 constant_dynamic-update-slice_fusion.2
  401.0 0.6 dynamic_slice.53
  401.5 0.6 iota_compare_fusion.4
  402.2 1.9 fusion.39
  404.1 2.2 gather_fusion
  406.3 0.3 reshape.269
  406.8 1.3 constant_dynamic-slice_fusion.5
  408.1 17.5 %fusion.41 = (f32[2,8,256]{2,1,0:T(8,128)S(1)}, f32[2,8,256,2304]{2,3,1,0:T(8,128)}) fusion(bf16[256,2,8,128]{3,0,2,1:T(8,128)(2,1)S(1)} %bitcast.103, pred[256,2304]{0,1:T(8,128)(4,1)S(1)} %fusion.39, bf16[256,2,128]{2,0,1:T(8,128)(2,1)S(1)} %dynamic-slice_bitcast_fusion.2, bf16[2048,2,128]{2,0,1:T(8,128)(2,1)S(1)} %copy.60), kind=kOutput, calls=%fused_computation.50.clone.1 | convolution fusion | flops 2456029440 | bytes 40583168 | tf_op jit(solution)/shard_map/while/body/eval_jaxpr/sub | solution.py:83
  425.6 2.2 gather_fusion.1
  427.8 0.3 reshape.270
  428.1 0.8 copy.62
  429.1 13.3 %fusion.42 = bf16[2,128,8,256]{3,1,2,0:T(8,128)(2,1)S(1)} fusion(f32[2,8,256,2304]{2,3,1,0:T(8,128)} %get-tuple-element.232, f32[2,8,256]{2,1,0:T(8,128)S(1)} %get-tuple-element.233, bf16[256,2,128]{0,2,1:T(8,128)(2,1)S(1)} %bitcast.109, bf16[2048,2,128]{0,2,1:T(8,128)(2,1)S(1)} %copy.62), kind=kOutput, calls=%fused_computation.14.clone.1 | convolution fusion | flops 2437677056 | bytes 39993344 | tf_op jit(solution)/shard_map/while/body/eval_jaxpr/kgnm,mkd->nkgd/dot_general | solution.py:85
  442.4 0.6 copy.63
  443.0 1.0 constant_dynamic-update-slice_fusion.2
  (41 shorter events, 2.1 us)
Async XLA Ops:
  7.2 23.3 %copy-start.1 = (f32[256,1024]{1,0:T(8,128)S(1)}, f32[256,1024]{1,0:T(8,128)}, u32[]{:S(2)}) copy-start(f32[256,1024]{1,0:T(8,128)} %param.13) | copy-start | bytes 3145732
  7.2 154.2 %all-gather.6.cloned.1.call-start = ((), (), s32[]{:S(2)}) async-start(), calls=%async_computation.4 | async-start | bytes 4718592 | tf_op jit(solution)/shard_map/all_gather | solution.py:48
  30.4 138.8 %all-gather.4.cloned.1.call-start = ((), (), s32[]{:S(2)}) async-start(), calls=%async_computation.3 | async-start | bytes 4718592 | tf_op jit(solution)/shard_map/all_gather | solution.py:49
  48.3 271.8 %all-gather.8.cloned.1.call-start = ((), (), s32[]{:S(2)}) async-start(), calls=%async_computation.5 | async-start | bytes 37748736 | tf_op jit(solution)/shard_map/all_gather | solution.py:47
  160.0 0.7 copy-start.2
  350.2 7.7 %copy-start.3 = (s32[1,2,16]{2,1,0:T(2,128)S(1)}, s32[1,2,16]{2,1,0:T(2,128)}, u32[]{:S(2)}) copy-start(s32[1,2,16]{2,1,0:T(2,128)} %param.17) | copy-start | bytes 388
  354.1 3.7 copy-start
Sparse Core Ops, SparseCore 0:
  30.5 35.6 all-gather.5
  68.7 36.5 all-gather.3
  160.2 159.7 all-gather.7
where the time goes:
time: 451 us
  waiting for transfers between devices  140 us (31%)
  blocking collectives  135 us (30%)
  matrix products  103 us (23%)
  local copies, waits for them, and re-layouts  44 us (10%)
  between operations  13.9 us (3%)
  other arithmetic  13.8 us (3%)
    all_gather x1, waiting for transfers between devices, per_device(): lax.all_gather(slabs[0], 'rep', axis=0, tiled=True)  140 us
    all_to_all x1, blocking collectives, per_device(): lax.all_to_all(weights[0], 'tp', split_axis=1, concat_axis=0, tiled=True)  97.8 us
    sub x2, matrix products, one_sequence(): expons = jnp.exp(scores - maxima)  34.9 us
    dot_general x2, matrix products, one_sequence(): jnp.einsum('kgnm,mkd->nkgd', probs, all_values, preferred_element_type=jn...  26.5 us
    reshape x1, matrix products, per_device(): raw_query.reshape(TOK, kv_local * group_size, HEAD_DIM)  25.8 us
    all_to_all x1, blocking collectives, per_device(): lax.all_to_all(weights[1], 'tp', split_axis=1, concat_axis=0, tiled=True)  20.6 us
    all_to_all x1, blocking collectives, per_device(): lax.all_to_all(weights[2], 'tp', split_axis=1, concat_axis=0, tiled=True)  16.6 us
    dot_general x2, matrix products, per_device(): jnp.dot(tokens, piece, preferred_element_type=jnp.float32)  16.1 us
  transfers between devices with their start and end apart: 3, of which 1 were waited for; matrix products, arithmetic and copies ran while one was open for 8% of the time, Pallas kernels for 0%

commit v1 on v0

--- a/solution.py
+++ b/solution.py
@@ -39,7 +39,12 @@
         value_weight.astype(jnp.bfloat16),
     )
     slabs = (
-        lax.all_to_all(weights[0], "tp", split_axis=1, concat_axis=0, tiled=True),
+        jnp.concatenate(
+            lax.all_to_all(
+                jnp.stack(jnp.split(weights[0], lax.axis_size("tp"), axis=1)), "tp", 0, 0
+            ),
+            axis=0,
+        ),
         lax.all_to_all(weights[1], "tp", split_axis=1, concat_axis=0, tiled=True),
         lax.all_to_all(weights[2], "tp", split_axis=1, concat_axis=0, tiled=True),
     )

time: 451 us -> 436 us (0.967)
  local copies, waits for them, and re-layouts: 44 us -> 30.4 us
    reshape x1 -> x0, matrix products: 25.8 us -> none  [per_device(): raw_query.reshape(TOK, kv_local * group_size, HEAD_DIM)]
    dot_general x2 -> x3, matrix products: 16.1 us -> 40.2 us  [per_device(): jnp.dot(tokens, piece, preferred_element_type=jnp.float32)]
    unnamed x12 -> x11, local copies, waits for them, and re-layouts: 9.93 us -> 2.35 us
    all_to_all x1 -> x0, local copies, waits for them, and re-layouts: 6.28 us -> none  [per_device(): lax.all_to_all(weights[0], 'tp', split_axis=1, concat_axis=0, tiled=True)]
  transfers between devices with their start and end apart: 3 -> 3, of which waited for: 1 -> 1; matrix products, arithmetic and copies ran while one was open for 8% -> 6% of each run, Pallas kernels for 0% -> 0%
where the time goes in v1:
time: 436 us; the launch traced here: 435 us
  waiting for transfers between devices  140 us (32%)
  blocking collectives  133 us (31%)
  matrix products  102 us (23%)
  local copies, waits for them, and re-layouts  30.4 us (7%)
  other arithmetic  16.3 us (4%)
  between operations  13.9 us (3%)
    all_gather x1, waiting for transfers between devices, per_device(): lax.all_gather(slabs[0], 'rep', axis=0, tiled=True)  140 us
    all_to_all x1, blocking collectives, per_device(): lax.all_to_all(jnp.stack(jnp.split(weights[0], lax.axis_size('tp'), axis=...  95.4 us
    dot_general x3, matrix products, per_device(): jnp.dot(tokens, piece, preferred_element_type=jnp.float32)  40.2 us
    sub x2, matrix products, one_sequence(): expons = jnp.exp(scores - maxima)  34.9 us
    dot_general x2, matrix products, one_sequence(): jnp.einsum('kgnm,mkd->nkgd', probs, all_values, preferred_element_type=jn...  26.5 us
    all_to_all x1, blocking collectives, per_device(): lax.all_to_all(weights[1], 'tp', split_axis=1, concat_axis=0, tiled=True)  20.6 us
    all_to_all x1, blocking collectives, per_device(): lax.all_to_all(weights[2], 'tp', split_axis=1, concat_axis=0, tiled=True)  16.6 us
  transfers between devices with their start and end apart: 3, of which 1 were waited for; matrix products, arithmetic and copies ran while one was open for 6% of the time, Pallas kernels for 0%

profile of v1, /device:TPU:0, one launch (start us, length us, event | category | flops | bytes accessed | tf_op | source)
XLA Modules:
  0.0 435.2 jit_solution(7797684527547986202)
XLA Ops:
  7.2 1.5 copy.33
  8.7 20.6 %all_to_all.43 = bf16[256,4,256]{0,2,1:T(8,128)(2,1)S(1)} all-to-all(bf16[256,4,256]{0,2,1:T(8,128)(2,1)S(1)} %bitcast.116), channel_id=1, replica_groups=mesh['rep'=8,'tp'=4] {'tp'}, dimensions={1} | all-to-all | bytes 1048576 | tf_op jit(solution)/shard_map/all_to_all | solution.py:48
  29.4 1.0 copy.34
  30.7 16.6 %all_to_all.44 = bf16[256,4,256]{0,2,1:T(8,128)(2,1)S(1)} all-to-all(bf16[256,4,256]{0,2,1:T(8,128)(2,1)S(1)} %bitcast.117), channel_id=1, replica_groups=mesh['rep'=8,'tp'=4] {'tp'}, dimensions={1} | all-to-all | bytes 1048576 | tf_op jit(solution)/shard_map/all_to_all | solution.py:49
  47.3 1.0 copy.32
  48.3 4.2 convert_element_type.57
  52.5 0.3 slice_bitcast_fusion.3
  52.9 0.6 pad_maximum_fusion
  53.4 95.4 %all_to_all.45 = bf16[4,256,2048]{2,1,0:T(8,128)(2,1)} all-to-all(bf16[4,256,2048]{2,1,0:T(8,128)(2,1)S(1)} %pad_maximum_fusion), channel_id=1, replica_groups=mesh['rep'=8,'tp'=4] {'tp'}, dimensions={0} | all-to-all | bytes 8388608 | tf_op jit(solution)/shard_map/all_to_all | solution.py:43
  148.9 0.6 copy-done.2
  149.6 0.5 multiply_cosine_fusion
  150.1 7.2 %fusion.23 = f32[512,256]{0,1:T(8,128)S(1)} fusion(bf16[512,8192]{1,0:T(8,128)(2,1)} %param.10, bf16[8192,256]{1,0:T(8,128)(2,1)} %all-gather.6.cloned.1.call-done), kind=kOutput, calls=%fused_computation.56 | convolution fusion | flops 2147483648 | bytes 13107200 | tf_op jit(solution)/shard_map/dot_general | solution.py:57
  157.5 0.3 pad_maximum_fusion.3
  158.1 9.0 %convolution_convert_fusion = bf16[512,256]{1,0:T(8,128)(2,1)S(1)} fusion(bf16[512,8192]{1,0:T(8,128)(2,1)} %param.10, bf16[8192,256]{1,0:T(8,128)(2,1)} %all-gather.4.cloned.1.call-done), kind=kOutput, calls=%fused_computation.41 | convolution fusion | flops 2147614720 | bytes 12845056 | tf_op jit(solution)/shard_map/dot_general | solution.py:57
  167.1 0.8 reshape_reshape.3
  168.1 0.8 pad_maximum_fusion.2
  168.9 139.8 %all-gather.8.cloned.1.call-done = bf16[8192,2048]{1,0:T(8,128)(2,1)} async-done(((bf16[1024,2048]{1,0:T(8,128)(2,1)}), bf16[8192,2048]{1,0:T(8,128)(2,1)}) %all-gather.8.cloned.1.call-update) | async-done | bytes 33554448 | tf_op jit(solution)/shard_map/all_gather | solution.py:52
  308.7 24.0 %fusion.24 = f32[2048,512]{1,0:T(8,128)S(1)} fusion(bf16[8192,2048]{1,0:T(8,128)(2,1)} %all-gather.8.cloned.1.call-done, bf16[512,8192]{1,0:T(8,128)(2,1)} %param.10), kind=kOutput, calls=%fused_computation.57 | convolution fusion | flops 17179869184 | bytes 46137344 | tf_op jit(solution)/shard_map/dot_general | solution.py:57
  332.7 0.8 subtract_convert_fusion
  333.8 1.1 concatenate.37
  334.9 3.9 pad_maximum_fusion.1
  338.9 3.7 copy.37
  342.6 86.1 %while.12 = (s32[]{:T(128)}, bf16[2,256,2048]{2,1,0:T(8,128)(2,1)}, s32[2,16]{1,0:T(2,128)S(1)}, bf16[32,128,256]{2,1,0:T(8,128)(2,1)}, bf16[2,256,2,128]{3,2,1,...) while((s32[]{:T(128)}, bf16[2,256,2048]{2,1,0:T(8,128)(2,1)}, ...), condition=%wide.region_3.4_spmd, body=%wide.region_0.3_spmd.sunk | while | flops 4894894080 | bytes 100859848 | solution.py:93
  342.6 0.6 dynamic_slice.53
  343.2 0.6 iota_compare_fusion.4
  343.8 1.9 fusion.39
  345.7 2.2 gather_fusion
  347.9 0.3 reshape.270
  348.3 1.3 constant_dynamic-slice_fusion.5
  349.7 17.5 %fusion.41 = (f32[2,8,256]{2,1,0:T(8,128)S(1)}, f32[2,8,256,2304]{2,3,1,0:T(8,128)}) fusion(bf16[256,2,8,128]{3,0,2,1:T(8,128)(2,1)S(1)} %bitcast.111, pred[256,2304]{0,1:T(8,128)(4,1)S(1)} %fusion.39, bf16[256,2,128]{2,0,1:T(8,128)(2,1)S(1)} %dynamic-slice_bitcast_fusion.2, bf16[2048,2,128]{2,0,1:T(8,128)(2,1)S(1)} %copy.55), kind=kOutput, calls=%fused_computation.55.clone.1 | convolution fusion | flops 2456029440 | bytes 40583168 | tf_op jit(solution)/shard_map/while/body/eval_jaxpr/sub | solution.py:88
  367.1 2.2 gather_fusion.1
  369.3 0.3 reshape.271
  369.6 0.8 copy.57
  370.7 13.3 %fusion.42 = bf16[2,128,8,256]{3,1,2,0:T(8,128)(2,1)S(1)} fusion(f32[2,8,256,2304]{2,3,1,0:T(8,128)} %get-tuple-element.236, f32[2,8,256]{2,1,0:T(8,128)S(1)} %get-tuple-element.237, bf16[256,2,128]{0,2,1:T(8,128)(2,1)S(1)} %bitcast.115, bf16[2048,2,128]{0,2,1:T(8,128)(2,1)S(1)} %copy.57), kind=kOutput, calls=%fused_computation.14.clone.1 | convolution fusion | flops 2437677056 | bytes 39993344 | tf_op jit(solution)/shard_map/while/body/eval_jaxpr/kgnm,mkd->nkgd/dot_general | solution.py:90
  384.0 0.6 copy.58
  384.6 1.0 constant_dynamic-update-slice_fusion.2
  385.7 0.6 dynamic_slice.53
  386.2 0.6 iota_compare_fusion.4
  386.8 1.9 fusion.39
  388.7 2.2 gather_fusion
  391.0 0.3 reshape.270
  391.4 1.3 constant_dynamic-slice_fusion.5
  392.7 17.5 %fusion.41 = (f32[2,8,256]{2,1,0:T(8,128)S(1)}, f32[2,8,256,2304]{2,3,1,0:T(8,128)}) fusion(bf16[256,2,8,128]{3,0,2,1:T(8,128)(2,1)S(1)} %bitcast.111, pred[256,2304]{0,1:T(8,128)(4,1)S(1)} %fusion.39, bf16[256,2,128]{2,0,1:T(8,128)(2,1)S(1)} %dynamic-slice_bitcast_fusion.2, bf16[2048,2,128]{2,0,1:T(8,128)(2,1)S(1)} %copy.55), kind=kOutput, calls=%fused_computation.55.clone.1 | convolution fusion | flops 2456029440 | bytes 40583168 | tf_op jit(solution)/shard_map/while/body/eval_jaxpr/sub | solution.py:88
  410.2 2.2 gather_fusion.1
  412.7 0.8 copy.57
  413.7 13.3 %fusion.42 = bf16[2,128,8,256]{3,1,2,0:T(8,128)(2,1)S(1)} fusion(f32[2,8,256,2304]{2,3,1,0:T(8,128)} %get-tuple-element.236, f32[2,8,256]{2,1,0:T(8,128)S(1)} %get-tuple-element.237, bf16[256,2,128]{0,2,1:T(8,128)(2,1)S(1)} %bitcast.115, bf16[2048,2,128]{0,2,1:T(8,128)(2,1)S(1)} %copy.57), kind=kOutput, calls=%fused_computation.14.clone.1 | convolution fusion | flops 2437677056 | bytes 39993344 | tf_op jit(solution)/shard_map/while/body/eval_jaxpr/kgnm,mkd->nkgd/dot_general | solution.py:90
  427.0 0.6 copy.58
  427.7 1.0 constant_dynamic-update-slice_fusion.2
  (42 shorter events, 2.4 us)
Async XLA Ops:
  7.2 23.3 %copy-start.1 = (f32[256,1024]{1,0:T(8,128)S(1)}, f32[256,1024]{1,0:T(8,128)}, u32[]{:S(2)}) copy-start(f32[256,1024]{1,0:T(8,128)} %param.13) | copy-start | bytes 3145732
  7.2 143.0 %all-gather.6.cloned.1.call-start = ((), (), s32[]{:S(2)}) async-start(), calls=%async_computation.4 | async-start | bytes 4718592 | tf_op jit(solution)/shard_map/all_gather | solution.py:53
  30.4 127.7 %all-gather.4.cloned.1.call-start = ((), (), s32[]{:S(2)}) async-start(), calls=%async_computation.3 | async-start | bytes 4718592 | tf_op jit(solution)/shard_map/all_gather | solution.py:54
  48.3 260.4 %all-gather.8.cloned.1.call-start = ((), (), s32[]{:S(2)}) async-start(), calls=%async_computation.5 | async-start | bytes 37748736 | tf_op jit(solution)/shard_map/all_gather | solution.py:52
  148.8 0.7 copy-start.2
  334.9 7.7 %copy-start.3 = (s32[1,2,16]{2,1,0:T(2,128)S(1)}, s32[1,2,16]{2,1,0:T(2,128)}, u32[]{:S(2)}) copy-start(s32[1,2,16]{2,1,0:T(2,128)} %param.17) | copy-start | bytes 388
  338.9 3.7 copy-start
Sparse Core Ops, SparseCore 0:
  30.5 35.6 all-gather.5
  68.7 36.5 all-gather.3
  149.0 159.7 all-gather.7
